TPU v7x, 32 devices: a whole 2x2x4 slice. The times are simulated.
32 devices in a mesh: gx: 4 (over y, x), gy: 4 (over z), gz: 2 (over core).
Axes of the slice: x: 2, y: 2, z: 4, core: 2. Of those that a mesh axis runs over, the one named last changes fastest.
Arguments:
- token_grad: bfloat16 [32768, 320], P(('gx', 'gy', 'gz')), may hold values from -6 to 6
- token_owner: int32 [32768, 1], P(('gx', 'gy', 'gz')), may hold values from 0 to 31; in each aligned block of 1024 rows (0 to 1023, 1024 to 2047, ...) at most 64 rows name the same one
- token_row: int32 [32768], P(('gx', 'gy', 'gz')), may hold values from 0 to 4095
- table: float32 [131072, 320], P(('gx', 'gy', 'gz')), may hold values from -6 to 6
- accum: float32 [131072], P(('gx', 'gy', 'gz')), may hold values from 0.1 to 10
Outputs:
- new_table: float32 [131072, 320], P(('gx', 'gy', 'gz'))
- new_accum: float32 [131072], P(('gx', 'gy', 'gz'))
- fresh_rows: bfloat16 [32768, 320], P(('gx', 'gy', 'gz'))
Inputs may be any that keep to these rules, and one draw needn't show every extreme that they name: `token_owner`: among the 1024 tokens of one device no owner is named by more than 64 tokens.
All inputs are finite; a program needn't handle non-finite values.
Results may differ from a plain program's by a relative error of at most 0.001.
Values may be sent and summed in bfloat16 or wider, within the bound.
A program may use at most 64 MiB of HBM per device.

v0:
```python
import jax
import jax.numpy as jnp
from jax import lax
from jax.sharding import PartitionSpec as P


def body(token_grad, token_owner, token_row, table, accum):
    devices = lax.axis_size(("gx", "gy", "gz"))
    token_count = token_grad.shape[0]
    width = token_grad.shape[1]
    rows_dev = table.shape[0]
    capacity = max(2, 2 * token_count // devices)
    slot_count = devices * capacity
    owners = token_owner[:, 0]
    matches = owners[:, None] == jnp.arange(devices, dtype=jnp.int32)[None, :]
    earlier = (jnp.arange(token_count)[:, None] > jnp.arange(token_count)[None, :]).astype(
        jnp.bfloat16
    )
    before = jnp.dot(earlier, matches.astype(jnp.bfloat16), preferred_element_type=jnp.float32)
    order_rank = jnp.sum(jnp.where(matches, before, 0.0), axis=1).astype(jnp.int32)
    target = owners * capacity + order_rank
    placer = jnp.arange(slot_count, dtype=jnp.int32)[:, None] == target[None, :]
    placer_bf = placer.astype(jnp.bfloat16)
    send_grad = jnp.dot(placer_bf, token_grad, preferred_element_type=jnp.float32).astype(
        jnp.bfloat16
    )
    send_row = jnp.max(jnp.where(placer, token_row[None, :], -1), axis=1)
    recv_grad, recv_row = (
        lax.all_to_all(
            send_grad.reshape(devices, capacity, width),
            ("gx", "gy", "gz"),
            split_axis=0,
            concat_axis=0,
            tiled=True,
        ),
        lax.all_to_all(
            send_row.reshape(devices, capacity),
            ("gx", "gy", "gz"),
            split_axis=0,
            concat_axis=0,
            tiled=True,
        ),
    )
    recv_grad = recv_grad.reshape(slot_count, width)
    recv_row = recv_row.reshape(slot_count)
    onehot = (jnp.arange(rows_dev, dtype=jnp.int32)[:, None] == recv_row[None, :]).astype(
        jnp.bfloat16
    )
    grad_sum = jnp.dot(onehot, recv_grad, preferred_element_type=jnp.float32)
    new_accum = accum + jnp.mean(grad_sum * grad_sum, axis=1)
    new_table = table - 0.5 * grad_sum / (jnp.sqrt(new_accum) + 1e-08)[:, None]
    answer_rows = jnp.take(new_table, jnp.maximum(recv_row, 0), axis=0).astype(jnp.bfloat16)
    returned = lax.all_to_all(
        answer_rows.reshape(devices, capacity, width),
        ("gx", "gy", "gz"),
        split_axis=0,
        concat_axis=0,
        tiled=True,
    )
    returned = returned.reshape(slot_count, width)
    fresh_rows = jnp.dot(placer_bf.T, returned, preferred_element_type=jnp.float32).astype(
        jnp.bfloat16
    )
    return (new_table, new_accum, fresh_rows)


def solution(mesh):
    return jax.shard_map(
        body,
        mesh=mesh,
        in_specs=(
            P(("gx", "gy", "gz"), None),
            P(("gx", "gy", "gz"), None),
            P(("gx", "gy", "gz")),
            P(("gx", "gy", "gz"), None),
            P(("gx", "gy", "gz")),
        ),
        out_specs=(P(("gx", "gy", "gz"), None), P(("gx", "gy", "gz")), P(("gx", "gy", "gz"), None)),
        check_vma=False,
    )
```

profile of v0, /device:TPU:0, one launch (start us, length us, event | category | flops | bytes accessed | tf_op | source)
XLA Modules:
  0.0 131.2 jit_solution(9367710173328653482)
XLA Ops:
  0.6 0.0 copy-start
  0.6 1.3 fusion.10
  2.0 0.7 convert_add_fusion
  2.6 1.9 %select_reduce_fusion = s32[2048]{0:T(1024)S(1)} fusion(s32[1024]{0:T(1024)} %param.7, s32[1024]{0:T(1024)S(1)} %convert_add_fusion), kind=kLoop, calls=%fused_computation.4 | loop fusion | flops 6289408 | bytes 16384 | tf_op jit(solution)/shard_map/reduce_max | solution.py:27
  4.5 0.7 all_to_all.12
  5.2 7.3 %all-to-all-start = ((s32[32,1,64]{2,1,0:T(1,128)}), s32[32,1,64]{2,1,0:T(1,128)S(1)}, u32[]{:S(2)}, u32[]{:S(2)}) async-start(s32[32,1,64]{2,1,0:T(1,128)} %all_to_all.12), calls=%async_computation | async-start | bytes 32768 | tf_op jit(solution)/shard_map/all_to_all | solution.py:36
  12.5 0.0 copy-done
  12.6 1.8 %fusion.7 = bf16[2048,320]{0,1:T(8,128)(2,1)S(1)} fusion(bf16[1024,320]{0,1:T(8,128)(2,1)S(1)} %copy-done, s32[1024]{0:T(1024)S(1)} %convert_add_fusion), kind=kOutput, calls=%fused_computation.15 | convolution fusion | flops 1344929792 | bytes 1970176 | tf_op jit(solution)/shard_map/dot_general | solution.py:24
  14.3 1.6 %copy.16 = bf16[2048,320]{1,0:T(8,128)(2,1)} copy(bf16[2048,320]{0,1:T(8,128)(2,1)S(1)} %fusion.7) | data formatting | bytes 2621440 | tf_op jit(solution)/shard_map/convert_element_type | solution.py:24
  15.9 3.8 %all-to-all-done = s32[32,1,64]{2,1,0:T(1,128)S(1)} async-done(((s32[32,1,64]{2,1,0:T(1,128)}), s32[32,1,64]{2,1,0:T(1,128)S(1)}, u32[]{:S(2)}, u32[]{:S(2)}) %all-to-all-start) | async-done | bytes 8224 | tf_op jit(solution)/shard_map/all_to_all | solution.py:36
  19.6 2.7 %all-to-all-start.1 = ((bf16[32,64,320]{2,1,0:T(8,128)(2,1)}), bf16[32,64,320]{2,1,0:T(8,128)(2,1)S(1)}, u32[]{:S(2)}, u32[]{:S(2)}) async-start(bf16[32,64,320]{2,1,0:T(8,128)(2,1)} %bitcast.1), calls=%async_computation.1 | async-start | bytes 3145728 | tf_op jit(solution)/shard_map/all_to_all | solution.py:29
  22.3 0.5 broadcast.42
  22.9 0.7 reduce.3
  23.5 0.1 eq.48
  23.6 0.1 reshape.69
  23.7 37.4 %all-to-all-done.1 = bf16[32,64,320]{2,1,0:T(8,128)(2,1)S(1)} async-done(((bf16[32,64,320]{2,1,0:T(8,128)(2,1)}), bf16[32,64,320]{2,1,0:T(8,128)(2,1)S(1)}, u32[]{:S(2)}, u32[]{:S(2)}) %all-to-all-start.1) | async-done | bytes 1310752 | tf_op jit(solution)/shard_map/all_to_all | solution.py:29
  61.1 0.0 slice-start
  61.1 0.0 copy-start.1
  61.1 0.0 slice-start.1
  61.1 7.5 %multiply_reduce_fusion = (f32[4096]{0:T(1024)S(1)}, f32[4096,320]{0,1:T(8,128)S(1)}) fusion(bf16[2048,320]{1,0:T(8,128)(2,1)S(1)} %bitcast.16, s32[2048]{0:T(1024)S(1)} %eq.48), kind=kOutput, calls=%fused_computation.9 | convolution fusion | flops 5379715072 | bytes 6578176 | tf_op jit(solution)/shard_map/dot_general | solution.py:49
  68.6 0.0 copy-done.1
  68.6 0.6 sqrt_add_fusion
  69.2 0.0 slice-done
  69.2 0.0 slice-done.1
  69.2 3.3 %divide_subtract_fusion = f32[4096,320]{0,1:T(8,128)} fusion(f32[4096,320]{0,1:T(8,128)S(1)} %bitcast.15, f32[4096,320]{0,1:T(8,128)S(1)} %get-tuple-element.6, f32[4096]{0:T(1024)S(1)} %get-tuple-element.3), kind=kLoop, calls=%fused_computation.8 | loop fusion | flops 3932160 | bytes 15745024 | tf_op jit(solution)/shard_map/sub | solution.py:51
  72.5 5.1 %copy.18 = bf16[4096,320]{1,0:T(8,128)(2,1)} copy(f32[4096,320]{0,1:T(8,128)} %divide_subtract_fusion) | data formatting | bytes 7864320 | tf_op jit(solution)/shard_map/sub | solution.py:51
  77.6 9.5 %gather_fusion = bf16[2048,320]{1,0:T(8,128)(2,1)S(1)} fusion(bf16[4096,320]{1,0:T(8,128)(2,1)} %copy.18, s32[2048]{0:T(1024)S(1)} %broadcast_clamp_fusion), kind=kCustom, calls=%fused_computation | custom fusion | bytes 2629632 | tf_op jit(solution)/shard_map/jit(_take)/gather | solution.py:52
  87.1 0.7 select_convert_fusion
  87.8 40.7 %all_to_all.19 = bf16[32,64,320]{2,1,0:T(8,128)(2,1)S(1)} all-to-all(bf16[32,64,320]{2,1,0:T(8,128)(2,1)S(1)} %select_convert_fusion), channel_id=1, replica_groups=mesh['gx'=4,'gy'=4,'gz'=2] {'gx','gy','gz'}, dimensions={0} | all-to-all | bytes 2621440 | tf_op jit(solution)/shard_map/all_to_all | solution.py:53
  128.5 2.7 %fusion.8 = bf16[1024,320]{0,1:T(8,128)(2,1)} fusion(bf16[2048,320]{1,0:T(8,128)(2,1)S(1)} %bitcast.17, s32[1024]{0:T(1024)S(1)} %convert_add_fusion), kind=kOutput, calls=%fused_computation.16 | convolution fusion | flops 1344602112 | bytes 1970176 | tf_op jit(solution)/shard_map/dot_general | solution.py:61
  (4 shorter events, 0.0 us)
Async XLA Ops:
  0.6 11.9 %copy-start = (bf16[1024,320]{0,1:T(8,128)(2,1)S(1)}, bf16[1024,320]{0,1:T(8,128)(2,1)}, u32[]{:S(2)}) copy-start(bf16[1024,320]{0,1:T(8,128)(2,1)} %param.5) | copy-start | bytes 1966084
  5.2 14.4 %all-to-all-start = ((s32[32,1,64]{2,1,0:T(1,128)}), s32[32,1,64]{2,1,0:T(1,128)S(1)}, u32[]{:S(2)}, u32[]{:S(2)}) async-start(s32[32,1,64]{2,1,0:T(1,128)} %all_to_all.12), calls=%async_computation | async-start | bytes 32768 | tf_op jit(solution)/shard_map/all_to_all | solution.py:36
  19.6 41.4 %all-to-all-start.1 = ((bf16[32,64,320]{2,1,0:T(8,128)(2,1)}), bf16[32,64,320]{2,1,0:T(8,128)(2,1)S(1)}, u32[]{:S(2)}, u32[]{:S(2)}) async-start(bf16[32,64,320]{2,1,0:T(8,128)(2,1)} %bitcast.1), calls=%async_computation.1 | async-start | bytes 3145728 | tf_op jit(solution)/shard_map/all_to_all | solution.py:29
  61.1 8.1 %slice-start = ((s8[5242880]{0:T(1024)(128)(4,1)}), s8[4194304]{0:T(1024)(128)(4,1)S(1)}, s32[]{:S(2)}) async-start(s8[5242880]{0:T(1024)(128)(4,1)} %bitcast.14), calls=%async_computation.3 | async-start | bytes 8388608
  61.1 7.5 %copy-start.1 = (f32[4096]{0:T(1024)S(1)}, f32[4096]{0:T(1024)}, u32[]{:S(2)}) copy-start(f32[4096]{0:T(1024)} %param.9) | copy-start | bytes 49156
  61.1 8.1 %slice-start.1 = ((s8[5242880]{0:T(1024)(128)(4,1)}), s8[1048576]{0:T(1024)(128)(4,1)S(1)}, s32[]{:S(2)}) async-start(s8[5242880]{0:T(1024)(128)(4,1)} %bitcast.14), calls=%async_computation.4 | async-start | bytes 2097152
where the time goes:
time: 132 us; the launch traced here: 131 us
  waiting for transfers between devices  41.1 us (31%)
  blocking collectives  40.7 us (31%)
  local copies, waits for them, and re-layouts  17.5 us (13%)
  matrix products  13.3 us (10%)
  starting transfers between devices  10 us (8%)
  other arithmetic  7.81 us (6%)
    all_to_all x1, blocking collectives, body(): lax.all_to_all(answer_rows.reshape(devices, capacity, width), ('gx', 'gy'...  40.7 us
    all_to_all x1, waiting for transfers between devices, body(): lax.all_to_all(send_grad.reshape(devices, capacity, width), ('gx', 'gy',...  37.4 us
    gather x1, local copies, waits for them, and re-layouts, body(): jnp.take(new_table, jnp.maximum(recv_row, 0), axis=0).astype(jnp.bfloat16)  9.49 us
    dot_general x1, matrix products, body(): grad_sum = jnp.dot(onehot, recv_grad, preferred_element_type=jnp.float32)  7.5 us
    all_to_all x1, starting transfers between devices, body(): lax.all_to_all(send_row.reshape(devices, capacity), ('gx', 'gy', 'gz'), s...  7.32 us
    sub x1, local copies, waits for them, and re-layouts, body(): new_table = table - 0.5 * grad_sum / (jnp.sqrt(new_accum) + 1e-08)[:, None]  5.11 us
    all_to_all x1, waiting for transfers between devices, body(): lax.all_to_all(send_row.reshape(devices, capacity), ('gx', 'gy', 'gz'), s...  3.76 us
    sub x1, other arithmetic, body(): new_table = table - 0.5 * grad_sum / (jnp.sqrt(new_accum) + 1e-08)[:, None]  3.27 us
  transfers between devices with their start and end apart: 2, of which 2 were waited for; matrix products, arithmetic and copies ran while one was open for 4% of the time, Pallas kernels for 0%

commit v1 on v0

v1 whole, which is shorter than its diff:
```python
import functools

import jax
import jax.numpy as jnp
from jax import lax
from jax.experimental import pallas as pl
from jax.experimental.pallas import tpu as pltpu
from jax.sharding import PartitionSpec as P

AXES = ("gx", "gy", "gz")
BF, F32 = jnp.bfloat16, jnp.float32
MESH = pl.DeviceIdType.MESH


def iota(shape, axis):
    return lax.broadcasted_iota(jnp.int32, shape, axis).astype(F32)


def floor_div(value, by):
    return jnp.floor((value + 0.5) * (1.0 / by))


def onehot(column, line):
    return jnp.where(column == line, 1.0, 0.0).astype(BF)


def nt(left, right):
    return lax.dot_general(left, right, (((1,), (1,)), ((), ())), preferred_element_type=F32)


def kernel(sizes, half, grad_ref, owner_ref, row_ref, table_ref, accum_ref,
           new_table_ref, new_accum_ref, fresh_ref,
           ext_a, ext_b, send, recv, total, table, new_table, new_a, new_b,
           lhs, ans_a, ans_b, answer, returned, fresh,
           send_sem, recv_sem, back_sem, ret_sem, table_sem, out_sem):
    xs, ys, zs = sizes
    n = xs * ys * zs
    width, tokens = grad_ref.shape
    rows = table.shape[1]
    main = width // 128 * 128
    tail = width - main
    group = max(1, 256 // half)
    groups = n // group
    gs = group * half
    step_self = (ys - 1) * xs * zs
    me = tuple(lax.axis_index(axis) for axis in AXES)

    def delta(step):
        b = ys - 1 - step // (xs * zs)
        return lax.rem(step // zs, xs), b, lax.rem(step, zs)

    def ahead(step):
        return tuple(lax.rem(m + d, s) for m, d, s in zip(me, delta(step), sizes))

    def behind(step):
        return tuple(lax.rem(m + s - d, s) for m, d, s in zip(me, delta(step), sizes))

    barrier = pltpu.get_barrier_semaphore()

    def greet(step, carry):
        @pl.when(step != step_self)
        def _():
            pl.semaphore_signal(barrier, inc=1, device_id=ahead(step), device_id_type=MESH)
        return carry

    lax.fori_loop(0, n, greet, 0)
    load = pltpu.make_async_copy(table_ref, table, table_sem)
    load.start()

    owner = owner_ref[...].astype(F32)
    step = iota((n, tokens), 0)
    b_part = floor_div(step, xs * zs)
    rest = step - b_part * (xs * zs)
    a_part = floor_div(rest, zs)
    c_part = rest - a_part * zs
    b_part = ys - 1 - b_part

    def turn(part, m, size):
        moved = part + m.astype(F32)
        return jnp.where(moved >= size, moved - size, moved)

    named = (turn(a_part, me[0], xs) * ys + turn(b_part, me[1], ys)) * zs + turn(c_part, me[2], zs)
    match = jnp.where(named == owner, 1.0, 0.0)
    earlier = jnp.where(iota((tokens, tokens), 0) < iota((tokens, tokens), 1), 1.0, 0.0).astype(BF)
    before = jnp.dot(match.astype(BF), earlier, preferred_element_type=F32)
    rank = jnp.sum(match * before, axis=0, keepdims=True)
    base = jnp.sum(match * step, axis=0, keepdims=True) * half
    in_a = rank < half
    pos_a = jnp.where(in_a, base + rank, -1.0)
    pos_b = jnp.where(in_a, -1.0, base + rank - half)

    row = row_ref[...].astype(F32) + 1.0
    high = floor_div(row, 128)
    low = row - high * 128
    where_row = lax.broadcasted_iota(jnp.int32, (128, tokens), 0)
    zeros = jnp.zeros((128 - tail, tokens), BF)
    for ext, first in ((ext_a, 0), (ext_b, 2)):
        ext[:main, :] = grad_ref[:main, :]
        ext[main + 128:, :] = jnp.where(
            where_row == first, high, jnp.where(where_row == first + 1, low, 0.0)).astype(BF)
    ext_a[main:main + tail, :] = grad_ref[main:, :]
    ext_a[main + tail:main + 128, :] = zeros
    ext_b[main:main + 128 - tail, :] = zeros
    ext_b[main + 128 - tail:main + 128, :] = grad_ref[main:, :]

    def place(g):
        line = iota((gs, 1), 0) + (g * gs).astype(F32)
        return onehot(line, pos_a), onehot(line, pos_b)

    def copy_out(step):
        return pltpu.make_async_remote_copy(
            src_ref=send.at[step], dst_ref=recv.at[step], send_sem=send_sem.at[step],
            recv_sem=recv_sem.at[step], device_id=ahead(step), device_id_type=MESH)

    def copy_back(step):
        return pltpu.make_async_remote_copy(
            src_ref=answer.at[step], dst_ref=returned.at[step], send_sem=back_sem.at[step],
            recv_sem=ret_sem.at[step], device_id=behind(step), device_id_type=MESH)

    def stay_out():
        return pltpu.make_async_copy(send.at[step_self], recv.at[step_self], recv_sem.at[step_self])

    def stay_back():
        return pltpu.make_async_copy(
            answer.at[step_self], returned.at[step_self], ret_sem.at[step_self])

    def start_group(g, remote, local):
        def one(i, carry):
            step = g * group + i

            @pl.when(step != step_self)
            def _():
                remote(step).start()

            @pl.when(step == step_self)
            def _():
                local().start()
            return carry
        lax.fori_loop(0, group, one, 0)

    def wait_group(g, remote, local):
        def one(i, carry):
            step = g * group + i

            @pl.when(step != step_self)
            def _():
                remote(step).wait_recv()

            @pl.when(step == step_self)
            def _():
                local().wait()
            return carry
        lax.fori_loop(0, group, one, 0)

    def wait_sent(remote):
        def one(step, carry):
            @pl.when(step != step_self)
            def _():
                remote(step).wait_send()
            return carry
        lax.fori_loop(0, n, one, 0)

    pl.semaphore_wait(barrier, n - 1)

    def pack(buffer, g, part_a, part_b):
        span = pl.ds(g * group, group)
        buffer[span, :, 0:main] = part_a[:, :main].astype(BF).reshape(group, half, main)
        buffer[span, :, main:2 * main] = part_b[:, :main].astype(BF).reshape(group, half, main)
        both = part_a[:, main:] + part_b[:, main:]
        buffer[span, :, 2 * main:] = both.astype(BF).reshape(group, half, both.shape[1])

    def scatter(g, carry):
        place_a, place_b = place(g)
        pack(send, g, nt(place_a, ext_a[...]), nt(place_b, ext_b[...]))
        start_group(g, copy_out, stay_out)
        return carry

    lax.fori_loop(0, groups, scatter, 0)
    total[...] = jnp.zeros_like(total)
    fresh[...] = jnp.zeros_like(fresh)

    def load_lhs(buffer, g):
        block = buffer[pl.ds(g * group, group)]
        block = block.reshape(gs, block.shape[2])
        tails = block[:, 2 * main:2 * main + 128].T
        lhs[:main, :gs] = block[:, :main].T
        lhs[:main, gs:] = block[:, main:2 * main].T
        lhs[main:, :gs] = tails[:tail]
        lhs[main:, gs:] = tails[128 - tail:]

    def row_columns(g):
        block = recv[pl.ds(g * group, group), :, 2 * main + 128:]
        block = block.reshape(gs, 128).astype(F32)
        return (block[:, 0:1] * 128 + block[:, 1:2] - 1.0,
                block[:, 2:3] * 128 + block[:, 3:4] - 1.0)

    tile = 512

    def collect(g, carry):
        wait_group(g, copy_out, stay_out)
        load_lhs(recv, g)
        row_a, row_b = row_columns(g)

        def part(r, inner):
            span = pl.ds(pl.multiple_of(r * tile, tile), tile)
            line = iota((1, tile), 1) + (r * tile).astype(F32)
            hot = jnp.concatenate([onehot(row_a, line), onehot(row_b, line)], axis=0)
            total[:, span] += jnp.dot(lhs[...], hot, preferred_element_type=F32)
            return inner

        lax.fori_loop(0, rows // tile, part, 0)
        return carry

    lax.fori_loop(0, groups, collect, 0)
    load.wait()

    def update(r, carry):
        span = pl.ds(pl.multiple_of(r * tile, tile), tile)
        summed = total[:, span]
        grown = accum_ref[:, span] + jnp.sum(summed * summed, axis=0, keepdims=True) * (1.0 / width)
        new_accum_ref[:, span] = grown
        moved = table[:, span] - summed * (0.5 / (jnp.sqrt(grown) + 1e-08))
        new_table[:, span] = moved
        short = moved.astype(BF)
        zero = jnp.zeros((128 - tail, tile), BF)
        new_a[:main, span] = short[:main]
        new_b[:main, span] = short[:main]
        new_a[main:main + tail, span] = short[main:]
        new_a[main + tail:, span] = zero
        new_b[main:main + 128 - tail, span] = zero
        new_b[main + 128 - tail:, span] = short[main:]
        return carry

    lax.fori_loop(0, rows // tile, update, 0)
    store = pltpu.make_async_copy(new_table, new_table_ref, out_sem)
    store.start()

    def reply(g, carry):
        row_a, row_b = row_columns(g)
        ans_a[...] = jnp.zeros_like(ans_a)
        ans_b[...] = jnp.zeros_like(ans_b)

        def part(r, inner):
            span = pl.ds(pl.multiple_of(r * tile, tile), tile)
            line = iota((1, tile), 1) + (r * tile).astype(F32)
            ans_a[...] += nt(onehot(row_a, line), new_a[:, span])
            ans_b[...] += nt(onehot(row_b, line), new_b[:, span])
            return inner

        lax.fori_loop(0, rows // tile, part, 0)
        pack(answer, g, ans_a[...], ans_b[...])
        start_group(g, copy_back, stay_back)
        return carry

    lax.fori_loop(0, groups, reply, 0)

    def finish(g, carry):
        wait_group(g, copy_back, stay_back)
        load_lhs(returned, g)
        fresh[...] += jnp.dot(
            lhs[...], jnp.concatenate(place(g), axis=0), preferred_element_type=F32)
        return carry

    lax.fori_loop(0, groups, finish, 0)
    fresh_ref[...] = fresh[...].astype(BF)
    wait_sent(copy_out)
    wait_sent(copy_back)
    store.wait()


def body(token_grad, token_owner, token_row, table, accum):
    sizes = tuple(lax.axis_size(axis) for axis in AXES)
    n = sizes[0] * sizes[1] * sizes[2]
    tokens, width = token_grad.shape
    rows = table.shape[0]
    half = max(16, tokens // n)
    group = max(1, 256 // half)
    gs = group * half
    main = width // 128 * 128
    vmem = pl.BlockSpec(memory_space=pltpu.VMEM)
    hbm = pl.BlockSpec(memory_space=pl.ANY)
    dma = pltpu.SemaphoreType.DMA
    new_table, new_accum, fresh = pl.pallas_call(
        functools.partial(kernel, sizes, half),
        out_shape=(
            jax.ShapeDtypeStruct((width, rows), F32),
            jax.ShapeDtypeStruct((1, rows), F32),
            jax.ShapeDtypeStruct((width, tokens), BF),
        ),
        in_specs=[vmem, vmem, vmem, hbm, vmem],
        out_specs=(hbm, vmem, vmem),
        scratch_shapes=[
            pltpu.VMEM((main + 256, tokens), BF),
            pltpu.VMEM((main + 256, tokens), BF),
            pltpu.VMEM((n, half, 2 * main + 256), BF),
            pltpu.VMEM((n, half, 2 * main + 256), BF),
            pltpu.VMEM((width, rows), F32),
            pltpu.VMEM((width, rows), F32),
            pltpu.VMEM((width, rows), F32),
            pltpu.VMEM((main + 128, rows), BF),
            pltpu.VMEM((main + 128, rows), BF),
            pltpu.VMEM((width, 2 * gs), BF),
            pltpu.VMEM((gs, main + 128), F32),
            pltpu.VMEM((gs, main + 128), F32),
            pltpu.VMEM((n, half, 2 * main + 128), BF),
            pltpu.VMEM((n, half, 2 * main + 128), BF),
            pltpu.VMEM((width, tokens), F32),
            dma((n,)), dma((n,)), dma((n,)), dma((n,)), dma, dma,
        ],
        compiler_params=pltpu.CompilerParams(
            collective_id=0, has_side_effects=True, vmem_limit_bytes=63 * 1024 * 1024),
    )(token_grad.T, token_owner.reshape(1, tokens), token_row.reshape(1, tokens), table.T,
      accum.reshape(1, rows))
    return new_table.T, new_accum.reshape(rows), fresh.T


def solution(mesh):
    return jax.shard_map(
        body,
        mesh=mesh,
        in_specs=(P(AXES, None), P(AXES, None), P(AXES), P(AXES, None), P(AXES)),
        out_specs=(P(AXES, None), P(AXES), P(AXES, None)),
        check_vma=False,
    )
```

time: 132 us -> 96.6 us (0.73)
  the two profiles are of different devices: /device:TPU:0 before, /device:TPU:25 now
where the time goes in v1:
time: 96.6 us; the launch traced here: 96.5 us
  Pallas kernels  88.8 us (92%)
  local copies, waits for them, and re-layouts  6.97 us (7%)
    pallas_call x1, Pallas kernels, body(): pl.pallas_call(functools.partial(kernel, sizes, half), out_shape=(jax.Sha...  88.8 us
    unnamed x7, local copies, waits for them, and re-layouts  6.97 us

profile of v1, /device:TPU:25, one launch (start us, length us, event | category | flops | bytes accessed | tf_op | source)
XLA Modules:
  0.0 96.5 jit_solution(14596699291694374610)
XLA Ops:
  0.6 88.8 %shard_map.76 = (f32[320,4096]{1,0:T(8,128)}, f32[1,4096]{1,0:T(1,128)}, bf16[320,1024]{1,0:T(8,128)(2,1)}) custom-call(bf16[320,1024]{1,0:T(8,128)(2,1)} %bitcast.11, s32[1,1024]{1,0:T(1,128)} %bitcast.14, s32[1,1024]{1,0:T(1,128)} %bitcast.15, f32[320,4096]{1,0:T(8,128)} %bitcast.8, f32[1,4096]{1,0:T(1,128)} %bitcast.12), custom_call_target="tpu_custom_call" | custom-call | tf_op jit(solution)/shard_map/pallas_call | solution.py:283
  89.5 0.0 copy-start.1
  89.5 0.0 copy-start
  89.5 5.5 %copy.11 = f32[4096,320]{0,1:T(8,128)} copy(f32[4096,320]{0,1:T(8,128)} %bitcast.9) | data formatting | bytes 10485760
  95.0 0.0 copy-done.1
  95.0 0.6 copy.12
  95.6 0.0 copy-done
  95.6 0.8 copy.13
Async XLA Ops:
  89.5 5.5 %copy-start.1 = (f32[1,4096]{1,0:T(1,128)S(1)}, f32[1,4096]{1,0:T(1,128)}, u32[]{:S(2)}) copy-start(f32[1,4096]{1,0:T(1,128)} %get-tuple-element.7) | copy-start | bytes 49156
  89.5 6.1 %copy-start = (bf16[320,1024]{1,0:T(8,128)(2,1)S(1)}, bf16[320,1024]{1,0:T(8,128)(2,1)}, u32[]{:S(2)}) copy-start(bf16[320,1024]{1,0:T(8,128)(2,1)} %get-tuple-element.8) | copy-start | bytes 1966084

commit v2 on v1

--- a/solution.py
+++ b/solution.py
@@ -30,24 +30,24 @@
 
 def kernel(sizes, half, grad_ref, owner_ref, row_ref, table_ref, accum_ref,
            new_table_ref, new_accum_ref, fresh_ref,
-           ext_a, ext_b, send, recv, total, table, new_table, new_a, new_b,
-           lhs, ans_a, ans_b, answer, returned, fresh,
-           send_sem, recv_sem, back_sem, ret_sem, table_sem, out_sem):
+           ext, send_row, recv_row, send, recv, total, table, new_table, short_table,
+           lhs, ans, answer, returned, fresh,
+           row_out_sem, row_in_sem, send_sem, recv_sem, back_sem, ret_sem, table_sem, out_sem):
     xs, ys, zs = sizes
     n = xs * ys * zs
     width, tokens = grad_ref.shape
     rows = table.shape[1]
     main = width // 128 * 128
     tail = width - main
-    group = max(1, 256 // half)
+    group = max(1, 128 // half)
     groups = n // group
     gs = group * half
-    step_self = (ys - 1) * xs * zs
+    step_self = ys - 1
     me = tuple(lax.axis_index(axis) for axis in AXES)
 
     def delta(step):
-        b = ys - 1 - step // (xs * zs)
-        return lax.rem(step // zs, xs), b, lax.rem(step, zs)
+        b = ys - 1 - lax.rem(step, ys)
+        return lax.rem(step // (ys * zs), xs), b, lax.rem(step // ys, zs)
 
     def ahead(step):
         return tuple(lax.rem(m + d, s) for m, d, s in zip(me, delta(step), sizes))
@@ -69,11 +69,10 @@
 
     owner = owner_ref[...].astype(F32)
     step = iota((n, tokens), 0)
-    b_part = floor_div(step, xs * zs)
-    rest = step - b_part * (xs * zs)
+    rest = floor_div(step, ys)
+    b_part = ys - 1 - (step - rest * ys)
     a_part = floor_div(rest, zs)
     c_part = rest - a_part * zs
-    b_part = ys - 1 - b_part
 
     def turn(part, m, size):
         moved = part + m.astype(F32)
@@ -92,26 +91,31 @@
     row = row_ref[...].astype(F32) + 1.0
     high = floor_div(row, 128)
     low = row - high * 128
-    where_row = lax.broadcasted_iota(jnp.int32, (128, tokens), 0)
+    lane = jnp.where(iota((128, tokens), 0) == rank, 1.0, 0.0).astype(BF)
+    rows_out = nt((match * high).astype(BF), lane) * 128.0 + nt((match * low).astype(BF), lane)
+    send_row[...] = rows_out.reshape(n, 1, 128)
     zeros = jnp.zeros((128 - tail, tokens), BF)
-    for ext, first in ((ext_a, 0), (ext_b, 2)):
-        ext[:main, :] = grad_ref[:main, :]
-        ext[main + 128:, :] = jnp.where(
-            where_row == first, high, jnp.where(where_row == first + 1, low, 0.0)).astype(BF)
-    ext_a[main:main + tail, :] = grad_ref[main:, :]
-    ext_a[main + tail:main + 128, :] = zeros
-    ext_b[main:main + 128 - tail, :] = zeros
-    ext_b[main + 128 - tail:main + 128, :] = grad_ref[main:, :]
+    ext[:width, :] = grad_ref[...]
+    ext[width:, :] = zeros
 
     def place(g):
         line = iota((gs, 1), 0) + (g * gs).astype(F32)
-        return onehot(line, pos_a), onehot(line, pos_b)
+        return jnp.concatenate([onehot(line, pos_a), onehot(line, pos_b)], axis=0)
 
     def copy_out(step):
         return pltpu.make_async_remote_copy(
             src_ref=send.at[step], dst_ref=recv.at[step], send_sem=send_sem.at[step],
             recv_sem=recv_sem.at[step], device_id=ahead(step), device_id_type=MESH)
 
+    def copy_row(step):
+        return pltpu.make_async_remote_copy(
+            src_ref=send_row.at[step], dst_ref=recv_row.at[step], send_sem=row_out_sem.at[step],
+            recv_sem=row_in_sem.at[step], device_id=ahead(step), device_id_type=MESH)
+
+    def stay_row():
+        return pltpu.make_async_copy(
+            send_row.at[step_self], recv_row.at[step_self], row_in_sem.at[step_self])
+
     def copy_back(step):
         return pltpu.make_async_remote_copy(
             src_ref=answer.at[step], dst_ref=returned.at[step], send_sem=back_sem.at[step],
@@ -124,9 +128,9 @@
         return pltpu.make_async_copy(
             answer.at[step_self], returned.at[step_self], ret_sem.at[step_self])
 
-    def start_group(g, remote, local):
+    def start_range(first, count, remote, local):
         def one(i, carry):
-            step = g * group + i
+            step = first + i
 
             @pl.when(step != step_self)
             def _():
@@ -136,11 +140,11 @@
             def _():
                 local().start()
             return carry
-        lax.fori_loop(0, group, one, 0)
-
-    def wait_group(g, remote, local):
+        lax.fori_loop(0, count, one, 0)
+
+    def wait_range(first, count, remote, local):
         def one(i, carry):
-            step = g * group + i
+            step = first + i
 
             @pl.when(step != step_self)
             def _():
@@ -150,7 +154,7 @@
             def _():
                 local().wait()
             return carry
-        lax.fori_loop(0, group, one, 0)
+        lax.fori_loop(0, count, one, 0)
 
     def wait_sent(remote):
         def one(step, carry):
@@ -161,18 +165,19 @@
         lax.fori_loop(0, n, one, 0)
 
     pl.semaphore_wait(barrier, n - 1)
-
-    def pack(buffer, g, part_a, part_b):
+    start_range(0, n, copy_row, stay_row)
+
+    def pack(buffer, g, parts):
+        part_a, part_b = parts[:gs], parts[gs:]
         span = pl.ds(g * group, group)
         buffer[span, :, 0:main] = part_a[:, :main].astype(BF).reshape(group, half, main)
         buffer[span, :, main:2 * main] = part_b[:, :main].astype(BF).reshape(group, half, main)
-        both = part_a[:, main:] + part_b[:, main:]
+        both = part_a[:, main:] + pltpu.roll(part_b[:, main:], 128 - tail, axis=1)
         buffer[span, :, 2 * main:] = both.astype(BF).reshape(group, half, both.shape[1])
 
     def scatter(g, carry):
-        place_a, place_b = place(g)
-        pack(send, g, nt(place_a, ext_a[...]), nt(place_b, ext_b[...]))
-        start_group(g, copy_out, stay_out)
+        pack(send, g, nt(place(g), ext[...]))
+        start_range(g * group, group, copy_out, stay_out)
         return carry
 
     lax.fori_loop(0, groups, scatter, 0)
@@ -189,15 +194,23 @@
         lhs[main:, gs:] = tails[128 - tail:]
 
     def row_columns(g):
-        block = recv[pl.ds(g * group, group), :, 2 * main + 128:]
-        block = block.reshape(gs, 128).astype(F32)
-        return (block[:, 0:1] * 128 + block[:, 1:2] - 1.0,
-                block[:, 2:3] * 128 + block[:, 3:4] - 1.0)
-
-    tile = 512
+        block = recv_row[pl.ds(g * group, group)].reshape(group, 128)
+        high = floor_div(block, 128)
+        slot = iota((gs, group), 0)
+        pick = jnp.where(floor_div(slot, half) == iota((gs, group), 1), 1.0, 0.0).astype(BF)
+        spread = (jnp.dot(pick, high.astype(BF), preferred_element_type=F32) * 128.0
+                  + jnp.dot(pick, (block - high * 128).astype(BF), preferred_element_type=F32))
+        slot = iota((gs, 128), 0)
+        slot = slot - floor_div(slot, half) * half
+        lanes = iota((gs, 128), 1)
+        return tuple(
+            jnp.sum(jnp.where(lanes == slot + first, spread, 0.0), axis=1, keepdims=True) - 1.0
+            for first in (0, half))
+
+    tile = 2048
 
     def collect(g, carry):
-        wait_group(g, copy_out, stay_out)
+        wait_range(g * group, group, copy_out, stay_out)
         load_lhs(recv, g)
         row_a, row_b = row_columns(g)
 
@@ -211,6 +224,7 @@
         lax.fori_loop(0, rows // tile, part, 0)
         return carry
 
+    wait_range(0, n, copy_row, stay_row)
     lax.fori_loop(0, groups, collect, 0)
     load.wait()
 
@@ -223,12 +237,8 @@
         new_table[:, span] = moved
         short = moved.astype(BF)
         zero = jnp.zeros((128 - tail, tile), BF)
-        new_a[:main, span] = short[:main]
-        new_b[:main, span] = short[:main]
-        new_a[main:main + tail, span] = short[main:]
-        new_a[main + tail:, span] = zero
-        new_b[main:main + 128 - tail, span] = zero
-        new_b[main + 128 - tail:, span] = short[main:]
+        short_table[:width, span] = short
+        short_table[width:, span] = zero
         return carry
 
     lax.fori_loop(0, rows // tile, update, 0)
@@ -237,32 +247,32 @@
 
     def reply(g, carry):
         row_a, row_b = row_columns(g)
-        ans_a[...] = jnp.zeros_like(ans_a)
-        ans_b[...] = jnp.zeros_like(ans_b)
+        ans[...] = jnp.zeros_like(ans)
 
         def part(r, inner):
             span = pl.ds(pl.multiple_of(r * tile, tile), tile)
             line = iota((1, tile), 1) + (r * tile).astype(F32)
-            ans_a[...] += nt(onehot(row_a, line), new_a[:, span])
-            ans_b[...] += nt(onehot(row_b, line), new_b[:, span])
+            hot = jnp.concatenate([onehot(row_a, line), onehot(row_b, line)], axis=0)
+            ans[...] += nt(hot, short_table[:, span])
             return inner
 
         lax.fori_loop(0, rows // tile, part, 0)
-        pack(answer, g, ans_a[...], ans_b[...])
-        start_group(g, copy_back, stay_back)
+        pack(answer, g, ans[...])
+        start_range(g * group, group, copy_back, stay_back)
         return carry
 
     lax.fori_loop(0, groups, reply, 0)
 
     def finish(g, carry):
-        wait_group(g, copy_back, stay_back)
+        wait_range(g * group, group, copy_back, stay_back)
         load_lhs(returned, g)
         fresh[...] += jnp.dot(
-            lhs[...], jnp.concatenate(place(g), axis=0), preferred_element_type=F32)
+            lhs[...], place(g), preferred_element_type=F32)
         return carry
 
     lax.fori_loop(0, groups, finish, 0)
     fresh_ref[...] = fresh[...].astype(BF)
+    wait_sent(copy_row)
     wait_sent(copy_out)
     wait_sent(copy_back)
     store.wait()
@@ -274,7 +284,7 @@
     tokens, width = token_grad.shape
     rows = table.shape[0]
     half = max(16, tokens // n)
-    group = max(1, 256 // half)
+    group = max(1, 128 // half)
     gs = group * half
     main = width // 128 * 128
     vmem = pl.BlockSpec(memory_space=pltpu.VMEM)
@@ -290,22 +300,21 @@
         in_specs=[vmem, vmem, vmem, hbm, vmem],
         out_specs=(hbm, vmem, vmem),
         scratch_shapes=[
-            pltpu.VMEM((main + 256, tokens), BF),
-            pltpu.VMEM((main + 256, tokens), BF),
-            pltpu.VMEM((n, half, 2 * main + 256), BF),
-            pltpu.VMEM((n, half, 2 * main + 256), BF),
+            pltpu.VMEM((main + 128, tokens), BF),
+            pltpu.VMEM((n, 1, 128), F32),
+            pltpu.VMEM((n, 1, 128), F32),
+            pltpu.VMEM((n, half, 2 * main + 128), BF),
+            pltpu.VMEM((n, half, 2 * main + 128), BF),
             pltpu.VMEM((width, rows), F32),
             pltpu.VMEM((width, rows), F32),
             pltpu.VMEM((width, rows), F32),
             pltpu.VMEM((main + 128, rows), BF),
-            pltpu.VMEM((main + 128, rows), BF),
             pltpu.VMEM((width, 2 * gs), BF),
-            pltpu.VMEM((gs, main + 128), F32),
-            pltpu.VMEM((gs, main + 128), F32),
+            pltpu.VMEM((2 * gs, main + 128), F32),
             pltpu.VMEM((n, half, 2 * main + 128), BF),
             pltpu.VMEM((n, half, 2 * main + 128), BF),
             pltpu.VMEM((width, tokens), F32),
-            dma((n,)), dma((n,)), dma((n,)), dma((n,)), dma, dma,
+            dma((n,)), dma((n,)), dma((n,)), dma((n,)), dma((n,)), dma((n,)), dma, dma,
         ],
         compiler_params=pltpu.CompilerParams(
             collective_id=0, has_side_effects=True, vmem_limit_bytes=63 * 1024 * 1024),

time: 96.6 us -> 85.7 us (0.89)
  the two profiles are of different devices: /device:TPU:25 before, /device:TPU:0 now
where the time goes in v2:
time: 85.7 us; the launch traced here: 85.3 us
  Pallas kernels  77.6 us (91%)
  local copies, waits for them, and re-layouts  6.97 us (8%)
    pallas_call x1, Pallas kernels, body(): pl.pallas_call(functools.partial(kernel, sizes, half), out_shape=(jax.Sha...  77.6 us
    unnamed x7, local copies, waits for them, and re-layouts  6.97 us

profile of v2, /device:TPU:0, one launch (start us, length us, event | category | flops | bytes accessed | tf_op | source)
XLA Modules:
  0.0 85.3 jit_solution(16672993774731815129)
XLA Ops:
  0.6 77.6 %shard_map.76 = (f32[320,4096]{1,0:T(8,128)}, f32[1,4096]{1,0:T(1,128)}, bf16[320,1024]{1,0:T(8,128)(2,1)}) custom-call(bf16[320,1024]{1,0:T(8,128)(2,1)} %bitcast.11, s32[1,1024]{1,0:T(1,128)} %bitcast.14, s32[1,1024]{1,0:T(1,128)} %bitcast.15, f32[320,4096]{1,0:T(8,128)} %bitcast.8, f32[1,4096]{1,0:T(1,128)} %bitcast.12), custom_call_target="tpu_custom_call" | custom-call | tf_op jit(solution)/shard_map/pallas_call | solution.py:293
  78.3 0.0 copy-start.1
  78.3 0.0 copy-start
  78.3 5.5 %copy.11 = f32[4096,320]{0,1:T(8,128)} copy(f32[4096,320]{0,1:T(8,128)} %bitcast.9) | data formatting | bytes 10485760
  83.8 0.0 copy-done.1
  83.8 0.6 copy.12
  84.4 0.0 copy-done
  84.4 0.8 copy.13
Async XLA Ops:
  78.3 5.5 %copy-start.1 = (f32[1,4096]{1,0:T(1,128)S(1)}, f32[1,4096]{1,0:T(1,128)}, u32[]{:S(2)}) copy-start(f32[1,4096]{1,0:T(1,128)} %get-tuple-element.7) | copy-start | bytes 49156
  78.3 6.1 %copy-start = (bf16[320,1024]{1,0:T(8,128)(2,1)S(1)}, bf16[320,1024]{1,0:T(8,128)(2,1)}, u32[]{:S(2)}) copy-start(bf16[320,1024]{1,0:T(8,128)(2,1)} %get-tuple-element.8) | copy-start | bytes 1966084
